TPU v7x, 32 devices: a whole 2x2x4 slice. The times are simulated.
32 devices in a mesh: dp: 4 (over x, core), wide: 8 (over z, y).
Axes of the slice: x: 2, y: 2, z: 4, core: 2. Of those that a mesh axis runs over, the one named last changes fastest.
Arguments:
- streams: float32 [4, 4096, 2048], P(None, 'dp', 'wide'), may hold values from -8 to 8
- cotangent: float32 [4, 4096, 2048], P(None, 'dp', 'wide'), may hold values from -6 to 6
- w_query: bfloat16 [2048, 2048], P('dp', 'wide'), may hold values from -2 to 2
- w_key: bfloat16 [2048, 2048], P('dp', 'wide'), may hold values from -0.125 to 0.125
- w_value: bfloat16 [2048, 2048], P('dp', 'wide'), may hold values from -0.125 to 0.125
- w_out: bfloat16 [2048, 2048], P('wide', 'dp'), may hold values from -1 to 1
- w_gate: bfloat16 [2048, 8192], P('dp', 'wide'), may hold values from -0.125 to 0.125
- w_up: bfloat16 [2048, 8192], P('dp', 'wide'), may hold values from -0.125 to 0.125
- w_down: bfloat16 [8192, 2048], P('wide', 'dp'), may hold values from -0.0625 to 0.0625
- hyper: float32 [2, 4, 6], replicated, may hold values from 0.1 to 0.6
- doc_ids: int32 [4, 1024], P('dp'), may hold values from 0 to 3, never falling along the last dimension, each value on 1 to 512 neighbouring positions
- span_starts: int32 [4, 2], P('dp'), may hold values from 0 to 768, as said below
- span_lengths: int32 [4, 2], P('dp'), may hold values from 64 to 256
Outputs:
- out_streams: float32 [4, 4096, 2048], P(None, 'dp', 'wide')
- d_streams: float32 [4, 4096, 2048], P(None, 'dp', 'wide')
- grad_query: float32 [2048, 2048], P('dp', 'wide')
- grad_key: float32 [2048, 2048], P('dp', 'wide')
- grad_value: float32 [2048, 2048], P('dp', 'wide')
- grad_out: float32 [2048, 2048], P('wide', 'dp')
- grad_gate: float32 [2048, 8192], P('dp', 'wide')
- grad_up: float32 [2048, 8192], P('dp', 'wide')
- grad_down: float32 [8192, 2048], P('wide', 'dp')
- grad_hyper: float32 [2, 4, 6], replicated
- clip_scale: float32 [16], P('wide')
- query_clipped: float32 [2048, 2048], P('dp', 'wide')
- key_clipped: float32 [2048, 2048], P('dp', 'wide')
Inputs may be any that keep to these rules, and one draw needn't show every extreme that they name: `doc_ids`: each row's document numbers never fall; every document holds 1 to 512 tokens, and one holds exactly 512. `span_starts`: span k of a sequence starts and ends inside the k-th of 2 equal regions of the sequence.
All inputs are finite; a program needn't handle non-finite values.
Results may differ from a plain program's by a relative error of at most 0.018.
Values may be sent and summed in bfloat16 or wider, within the bound.
A program may use at most 192 MiB of HBM per device.

v0:
```python
import math
import jax
import jax.numpy as jnp
from jax import lax
from jax.sharding import PartitionSpec as P

D = 2048
H = 16
CLIP_TAU = 6
EPSILON = 1e-05
MASKED = -1e30


def rope_tables(length, head_size):
    half_size = head_size // 2
    inverse = 10000.0 ** (-2.0 * jnp.arange(half_size, dtype=jnp.float32) / head_size)
    angles = jnp.arange(length, dtype=jnp.float32)[:, None] * inverse[None, :]
    cosine_table = jnp.cos(angles)
    sine_table = jnp.sin(angles)
    return (
        jnp.concatenate([cosine_table, cosine_table], axis=1),
        jnp.concatenate([sine_table, sine_table], axis=1),
    )


def rotate(values, cosine_table, sine_table):
    half_size = values.shape[-1] // 2
    turned = jnp.concatenate([-values[..., half_size:], values[..., :half_size]], axis=-1)
    return values * cosine_table[:, None, :] + turned * sine_table[:, None, :]


def rotate_back(grads, cosine_table, sine_table):
    half_size = grads.shape[-1] // 2
    scaled = grads * sine_table[:, None, :]
    turned = jnp.concatenate([scaled[..., half_size:], -scaled[..., :half_size]], axis=-1)
    return grads * cosine_table[:, None, :] + turned


def mix_inputs(weights_in, stream_set):
    return jnp.sum(weights_in[:, None, None] * stream_set, axis=0)


def mix_streams(matrix, stream_set):
    return jnp.sum(matrix[:, :, None, None] * stream_set[None, :, :, :], axis=1)


def mix_back(matrix, grads):
    return jnp.sum(matrix[:, :, None, None] * grads[:, None, :, :], axis=0)


def hyper_rows(pre_grad, post_grad, mix_grad):
    return jnp.concatenate([pre_grad[:, None], post_grad[:, None], mix_grad], axis=1)


def span_labels(positions, starts, lengths):
    inside = (positions[:, None] >= starts[None, :]) & (
        positions[:, None] < (starts + lengths)[None, :]
    )
    numbers = jnp.arange(1, starts.shape[0] + 1, dtype=jnp.int32)
    return jnp.sum(jnp.where(inside, numbers[None, :], 0), axis=1)


def block_mask(doc_row, labels, start_row, count_rows):
    key_pos = jnp.arange(doc_row.shape[0], dtype=jnp.int32)
    query_pos = start_row + jnp.arange(count_rows, dtype=jnp.int32)
    query_docs = lax.dynamic_slice_in_dim(doc_row, start_row, count_rows)
    query_labels = lax.dynamic_slice_in_dim(labels, start_row, count_rows)
    same_doc = query_docs[:, None] == doc_row[None, :]
    causal = key_pos[None, :] <= query_pos[:, None]
    joint_span = (query_labels[:, None] > 0) & (query_labels[:, None] == labels[None, :])
    return same_doc & (causal | joint_span)


def attend_forward(queries, keys_roped, values, doc_row, starts, lengths, score_scale):
    length, head_count, head_size = queries.shape
    block_rows = min(512, length)
    labels = span_labels(jnp.arange(length, dtype=jnp.int32), starts, lengths)

    def one_block(block_index):
        start_row = block_index * block_rows
        query_rows = lax.dynamic_slice_in_dim(queries, start_row, block_rows, 0)
        scores = (
            jnp.einsum("qhd,khd->hqk", query_rows, keys_roped, preferred_element_type=jnp.float32)
            * score_scale
        )
        allowed = block_mask(doc_row, labels, start_row, block_rows)
        masked = jnp.where(allowed[None, :, :], scores, MASKED)
        largest = jnp.max(masked, axis=2)
        exponent = jnp.exp(masked - largest[:, :, None])
        totals = jnp.sum(exponent, axis=2)
        weights_low = (exponent / totals[:, :, None]).astype(jnp.bfloat16)
        attended = jnp.einsum(
            "hqk,khd->qhd", weights_low, values, preferred_element_type=jnp.float32
        )
        return (attended, largest + jnp.log(totals), jnp.max(largest, axis=1))

    attended, log_sums, block_tops = lax.map(
        one_block, jnp.arange(length // block_rows, dtype=jnp.int32)
    )
    return (attended.reshape(length, head_count, head_size), log_sums, jnp.max(block_tops, axis=0))


def attend_backward(
    queries, keys_roped, values, dout, log_sums, doc_row, starts, lengths, score_scale
):
    length, head_count, head_size = queries.shape
    block_rows = min(512, length)
    labels = span_labels(jnp.arange(length, dtype=jnp.int32), starts, lengths)

    def one_block(carry, inputs):
        key_grad, value_grad = carry
        block_index, log_rows = inputs
        start_row = block_index * block_rows
        query_rows = lax.dynamic_slice_in_dim(queries, start_row, block_rows, 0)
        dout_rows = lax.dynamic_slice_in_dim(dout, start_row, block_rows, 0)
        scores = (
            jnp.einsum("qhd,khd->hqk", query_rows, keys_roped, preferred_element_type=jnp.float32)
            * score_scale
        )
        allowed = block_mask(doc_row, labels, start_row, block_rows)
        masked = jnp.where(allowed[None, :, :], scores, MASKED)
        weights_full = jnp.where(allowed[None, :, :], jnp.exp(masked - log_rows[:, :, None]), 0.0)
        weight_grad = jnp.einsum(
            "qhd,khd->hqk", dout_rows, values, preferred_element_type=jnp.float32
        )
        centre = jnp.sum(weights_full * weight_grad, axis=2, keepdims=True)
        score_grad = (weights_full * (weight_grad - centre)).astype(jnp.bfloat16)
        query_grad = score_scale * jnp.einsum(
            "hqk,khd->qhd", score_grad, keys_roped, preferred_element_type=jnp.float32
        )
        key_grad = key_grad + score_scale * jnp.einsum(
            "hqk,qhd->khd", score_grad, query_rows, preferred_element_type=jnp.float32
        )
        value_grad = value_grad + jnp.einsum(
            "hqk,qhd->khd",
            weights_full.astype(jnp.bfloat16),
            dout_rows,
            preferred_element_type=jnp.float32,
        )
        return ((key_grad, value_grad), query_grad)

    empty_grad = jnp.zeros((length, head_count, head_size), jnp.float32)
    count_blocks = length // block_rows
    (key_grad, value_grad), query_grad = lax.scan(
        one_block, (empty_grad, empty_grad), (jnp.arange(count_blocks, dtype=jnp.int32), log_sums)
    )
    return (query_grad.reshape(length, head_count, head_size), key_grad, value_grad)


def row_sums(first_term, second_term):
    return lax.psum((jnp.sum(first_term, axis=1), jnp.sum(second_term, axis=1)), "wide")


def features(piece):
    return lax.all_gather(piece, "wide", axis=1, tiled=True)


def branch_rows(partial_value):
    return lax.psum_scatter(partial_value, "wide", scatter_dimension=1, tiled=True)


def norm_forward(hidden):
    local_width = hidden.shape[1]
    full_width = local_width * lax.axis_size("wide")
    row_total, squares = row_sums(hidden, hidden * hidden)
    centre = row_total / full_width
    spread = squares / full_width - centre * centre
    inverse = lax.rsqrt(spread + EPSILON)
    normed = (hidden - centre[:, None]) * inverse[:, None]
    return (features(normed.astype(jnp.bfloat16)), normed, inverse)


def norm_backward(partial_value, normed, inverse):
    full_width = partial_value.shape[1]
    grad_rows = lax.psum_scatter(partial_value, "wide", scatter_dimension=1, tiled=True)
    row_total, row_cross = row_sums(grad_rows, grad_rows * normed)
    return inverse[:, None] * (
        grad_rows - row_total[:, None] / full_width - normed * row_cross[:, None] / full_width
    )


def per_device(
    streams,
    cotangent,
    w_query,
    w_key,
    w_value,
    w_out,
    w_gate,
    w_up,
    w_down,
    hyper,
    doc_ids,
    span_starts,
    span_lengths,
):
    seq_count, length = doc_ids.shape
    tokens = streams.shape[1]
    head_size = D // H
    column_count = w_query.shape[1]
    head_count = column_count // head_size
    score_scale = 1.0 / math.sqrt(head_size)
    cosine_table, sine_table = rope_tables(length, head_size)
    shape_heads = (seq_count, length, head_count, head_size)
    attn_pre, attn_post, attn_mix = (hyper[0, :, 0], hyper[0, :, 1], hyper[0, :, 2:])
    ffn_pre, ffn_post, ffn_mix = (hyper[1, :, 0], hyper[1, :, 1], hyper[1, :, 2:])
    query_w, key_w, value_w, out_w = (
        lax.all_gather(w_query, "dp", axis=0, tiled=True),
        lax.all_gather(w_key, "dp", axis=0, tiled=True),
        lax.all_gather(w_value, "dp", axis=0, tiled=True),
        lax.all_gather(w_out, "dp", axis=1, tiled=True),
    )
    gate_w, up_w, down_w = (
        lax.all_gather(w_gate, "dp", axis=0, tiled=True),
        lax.all_gather(w_up, "dp", axis=0, tiled=True),
        lax.all_gather(w_down, "dp", axis=1, tiled=True),
    )
    normed_one, kept_one, inverse_one = norm_forward(mix_inputs(attn_pre, streams))
    query_raw = jnp.dot(normed_one, query_w, preferred_element_type=jnp.float32).reshape(
        shape_heads
    )
    key_raw = jnp.dot(normed_one, key_w, preferred_element_type=jnp.float32).reshape(shape_heads)
    values = (
        jnp.dot(normed_one, value_w, preferred_element_type=jnp.float32)
        .astype(jnp.bfloat16)
        .reshape(shape_heads)
    )
    queries = rotate(query_raw, cosine_table, sine_table).astype(jnp.bfloat16)
    keys_roped = rotate(key_raw, cosine_table, sine_table).astype(jnp.bfloat16)

    def forward_sequence(inputs):
        return attend_forward(
            inputs[0], inputs[1], inputs[2], inputs[3], inputs[4], inputs[5], score_scale
        )

    attended, log_sums, seq_tops = lax.map(
        forward_sequence, (queries, keys_roped, values, doc_ids, span_starts, span_lengths)
    )
    head_top = lax.pmax(jnp.max(seq_tops, axis=0), "dp")
    attended_low = attended.reshape(tokens, column_count).astype(jnp.bfloat16)
    branch_one = branch_rows(jnp.dot(attended_low, out_w, preferred_element_type=jnp.float32))
    after_attn = mix_streams(attn_mix, streams) + attn_post[:, None, None] * branch_one[None, :, :]
    normed_two, kept_two, inverse_two = norm_forward(mix_inputs(ffn_pre, after_attn))
    gate_proj = jnp.dot(normed_two, gate_w, preferred_element_type=jnp.float32)
    up_proj = jnp.dot(normed_two, up_w, preferred_element_type=jnp.float32)
    sigmoid_gate = jax.nn.sigmoid(gate_proj)
    hidden = (gate_proj * sigmoid_gate * up_proj).astype(jnp.bfloat16)
    branch_two = branch_rows(jnp.dot(hidden, down_w, preferred_element_type=jnp.float32))
    out_streams = (
        mix_streams(ffn_mix, after_attn) + ffn_post[:, None, None] * branch_two[None, :, :]
    )
    ffn_post_grad = jnp.sum(cotangent * branch_two[None, :, :], axis=(1, 2))
    ffn_mix_grad = jnp.sum(cotangent[:, None, :, :] * after_attn[None, :, :, :], axis=(2, 3))
    two_grad = features(jnp.sum(ffn_post[:, None, None] * cotangent, axis=0).astype(jnp.bfloat16))
    hidden_grad = jnp.dot(two_grad, down_w.T, preferred_element_type=jnp.float32)
    down_wgrad = jnp.einsum("tf,td->fd", hidden, two_grad, preferred_element_type=jnp.float32)
    gate_grad = (
        hidden_grad * up_proj * sigmoid_gate * (1.0 + gate_proj * (1.0 - sigmoid_gate))
    ).astype(jnp.bfloat16)
    up_grad = (hidden_grad * gate_proj * sigmoid_gate).astype(jnp.bfloat16)
    gate_wgrad = jnp.einsum("td,tf->df", normed_two, gate_grad, preferred_element_type=jnp.float32)
    up_wgrad = jnp.einsum("td,tf->df", normed_two, up_grad, preferred_element_type=jnp.float32)
    gate_shard, up_shard, down_shard = (
        lax.psum_scatter(gate_wgrad, "dp", scatter_dimension=0, tiled=True),
        lax.psum_scatter(up_wgrad, "dp", scatter_dimension=0, tiled=True),
        lax.psum_scatter(down_wgrad, "dp", scatter_dimension=1, tiled=True),
    )
    normed_two_grad = jnp.dot(gate_grad, gate_w.T, preferred_element_type=jnp.float32) + jnp.dot(
        up_grad, up_w.T, preferred_element_type=jnp.float32
    )
    h_two_grad = norm_backward(normed_two_grad, kept_two, inverse_two)
    ffn_pre_grad = jnp.sum(h_two_grad[None, :, :] * after_attn, axis=(1, 2))
    after_grad = mix_back(ffn_mix, cotangent) + ffn_pre[:, None, None] * h_two_grad[None, :, :]
    attn_post_grad = jnp.sum(after_grad * branch_one[None, :, :], axis=(1, 2))
    attn_mix_grad = jnp.sum(after_grad[:, None, :, :] * streams[None, :, :, :], axis=(2, 3))
    one_grad = features(jnp.sum(attn_post[:, None, None] * after_grad, axis=0).astype(jnp.bfloat16))
    attended_grad = jnp.dot(one_grad, out_w.T, preferred_element_type=jnp.float32).astype(
        jnp.bfloat16
    )
    out_wgrad = jnp.einsum("tc,td->cd", attended_low, one_grad, preferred_element_type=jnp.float32)

    def backward_sequence(inputs):
        return attend_backward(
            inputs[0],
            inputs[1],
            inputs[2],
            inputs[3],
            inputs[4],
            inputs[5],
            inputs[6],
            inputs[7],
            score_scale,
        )

    query_grad, key_grad, value_grad = lax.map(
        backward_sequence,
        (
            queries,
            keys_roped,
            values,
            attended_grad.reshape(shape_heads),
            log_sums,
            doc_ids,
            span_starts,
            span_lengths,
        ),
    )
    query_low = (
        rotate_back(query_grad, cosine_table, sine_table)
        .reshape(tokens, column_count)
        .astype(jnp.bfloat16)
    )
    key_low = (
        rotate_back(key_grad, cosine_table, sine_table)
        .reshape(tokens, column_count)
        .astype(jnp.bfloat16)
    )
    value_low = value_grad.reshape(tokens, column_count).astype(jnp.bfloat16)
    query_wgrad = jnp.einsum("td,tc->dc", normed_one, query_low, preferred_element_type=jnp.float32)
    key_wgrad = jnp.einsum("td,tc->dc", normed_one, key_low, preferred_element_type=jnp.float32)
    value_wgrad = jnp.einsum("td,tc->dc", normed_one, value_low, preferred_element_type=jnp.float32)
    normed_one_grad = (
        jnp.dot(query_low, query_w.T, preferred_element_type=jnp.float32)
        + jnp.dot(key_low, key_w.T, preferred_element_type=jnp.float32)
        + jnp.dot(value_low, value_w.T, preferred_element_type=jnp.float32)
    )
    h_one_grad = norm_backward(normed_one_grad, kept_one, inverse_one)
    attn_pre_grad = jnp.sum(h_one_grad[None, :, :] * streams, axis=(1, 2))
    streams_grad = mix_back(attn_mix, after_grad) + attn_pre[:, None, None] * h_one_grad[None, :, :]
    hyper_grad = lax.psum(
        jnp.stack(
            [
                hyper_rows(attn_pre_grad, attn_post_grad, attn_mix_grad),
                hyper_rows(ffn_pre_grad, ffn_post_grad, ffn_mix_grad),
            ]
        ),
        ("dp", "wide"),
    )
    query_shard, key_shard, value_shard, out_shard = (
        lax.psum_scatter(query_wgrad, "dp", scatter_dimension=0, tiled=True),
        lax.psum_scatter(key_wgrad, "dp", scatter_dimension=0, tiled=True),
        lax.psum_scatter(value_wgrad, "dp", scatter_dimension=0, tiled=True),
        lax.psum_scatter(out_wgrad, "dp", scatter_dimension=1, tiled=True),
    )
    clip_scale = jnp.sqrt(CLIP_TAU / jnp.maximum(head_top, CLIP_TAU))
    columns = jnp.repeat(clip_scale, head_size)[None, :]
    return (
        out_streams,
        streams_grad,
        query_shard,
        key_shard,
        value_shard,
        out_shard,
        gate_shard,
        up_shard,
        down_shard,
        hyper_grad,
        clip_scale,
        w_query.astype(jnp.float32) * columns,
        w_key.astype(jnp.float32) * columns,
    )


def solution(mesh):
    return jax.shard_map(
        per_device,
        mesh=mesh,
        in_specs=(
            P(None, "dp", "wide"),
            P(None, "dp", "wide"),
            P("dp", "wide"),
            P("dp", "wide"),
            P("dp", "wide"),
            P("wide", "dp"),
            P("dp", "wide"),
            P("dp", "wide"),
            P("wide", "dp"),
            P(),
            P("dp", None),
            P("dp", None),
            P("dp", None),
        ),
        out_specs=(
            P(None, "dp", "wide"),
            P(None, "dp", "wide"),
            P("dp", "wide"),
            P("dp", "wide"),
            P("dp", "wide"),
            P("wide", "dp"),
            P("dp", "wide"),
            P("dp", "wide"),
            P("wide", "dp"),
            P(),
            P("wide"),
            P("dp", "wide"),
            P("dp", "wide"),
        ),
        check_vma=False,
    )
```

profile of v0, /device:TPU:0, one launch (start us, length us, event | category | flops | bytes accessed | tf_op | source)
XLA Modules:
  0.0 1579.7 jit_solution(8456090871075567823)
XLA Ops:
  11.9 23.4 %all-reduce.3 = (f32[1024]{0:T(1024)S(1)}, f32[1024]{0:T(1024)S(1)}) all-reduce(f32[1024]{0:T(1024)S(1)} %multiply_reduce_fusion.20, f32[1024]{0:T(1024)S(1)} %get-tuple-element.312), channel_id=1, replica_groups=mesh['dp'=4,'wide'=8] {'wide'}, use_global_device_ids=true, to_apply=%region_5.6 | all-reduce | flops 2048 | bytes 16384 | tf_op jit(solution)/shard_map/psum | solution.py:151
  42.8 66.4 %all-gather.12.cloned.1.call-done = bf16[1024,2048]{1,0:T(8,128)(2,1)} async-done(((bf16[1024,256]{1,0:T(8,128)(2,1)}), bf16[1024,2048]{1,0:T(8,128)(2,1)}) %all-gather.12.cloned.1.call-update) | async-done | bytes 4194320 | tf_op jit(solution)/shard_map/all_gather | solution.py:155
  147.9 14.2 while.53
  175.5 141.2 %reduce-scatter.12.cloned.1.call-done = f32[1024,256]{1,0:T(8,128)} async-done(((f32[1024,2048]{1,0:T(8,128)}), f32[1024,256]{1,0:T(8,128)}) %reduce-scatter.12.cloned.1.call-update) | async-done | bytes 1048592 | tf_op jit(solution)/shard_map/reduce_scatter | solution.py:159
  322.2 19.7 %all-reduce.2 = (f32[1024]{0:T(1024)S(1)}, f32[1024]{0:T(1024)S(1)}) all-reduce(f32[1024]{0:T(1024)S(1)} %multiply_reduce_fusion.19, f32[1024]{0:T(1024)S(1)} %get-tuple-element.310), channel_id=1, replica_groups=mesh['dp'=4,'wide'=8] {'wide'}, use_global_device_ids=true, to_apply=%region_18.19 | all-reduce | flops 2048 | bytes 16384 | tf_op jit(solution)/shard_map/psum | solution.py:151
  351.8 77.3 %all-gather.22.cloned.1.call-done = bf16[1024,2048]{1,0:T(8,128)(2,1)} async-done(((bf16[1024,256]{1,0:T(8,128)(2,1)}), bf16[1024,2048]{1,0:T(8,128)(2,1)}) %all-gather.22.cloned.1.call-update) | async-done | bytes 4194320 | tf_op jit(solution)/shard_map/all_gather | solution.py:155
  439.1 24.3 %all-gather.26.cloned.1.call-done = bf16[2048,1024]{1,0:T(8,128)(2,1)} async-done(((bf16[512,1024]{1,0:T(8,128)(2,1)}), bf16[2048,1024]{1,0:T(8,128)(2,1)}) %all-gather.26.cloned.1.call-update) | async-done | bytes 4194320 | tf_op jit(solution)/shard_map/all_gather | solution.py:215
  475.4 23.8 %all-gather.28.cloned.1.call-done = bf16[1024,2048]{1,0:T(8,128)(2,1)} async-done(((bf16[1024,512]{1,0:T(8,128)(2,1)}), bf16[1024,2048]{1,0:T(8,128)(2,1)}) %all-gather.28.cloned.1.call-update) | async-done | bytes 4194320 | tf_op jit(solution)/shard_map/all_gather | solution.py:216
  520.7 137.2 %reduce-scatter.14.cloned.1.call-done = f32[1024,256]{1,0:T(8,128)} async-done(((f32[1024,2048]{1,0:T(8,128)}), f32[1024,256]{1,0:T(8,128)}) %reduce-scatter.14.cloned.1.call-update) | async-done | bytes 1048592 | tf_op jit(solution)/shard_map/reduce_scatter | solution.py:159
  666.3 73.4 %all-gather.30.cloned.1.call-done = bf16[1024,2048]{1,0:T(8,128)(2,1)} async-done(((bf16[1024,256]{1,0:T(8,128)(2,1)}), bf16[1024,2048]{1,0:T(8,128)(2,1)}) %all-gather.30.cloned.1.call-update) | async-done | bytes 4194320 | tf_op jit(solution)/shard_map/all_gather | solution.py:155
  739.7 12.9 multiply_convert_fusion.1
  766.6 146.1 %reduce-scatter.16.cloned.1.call-done = f32[1024,256]{1,0:T(8,128)} async-done(((f32[1024,2048]{1,0:T(8,128)}), f32[1024,256]{1,0:T(8,128)}) %reduce-scatter.16.cloned.1.call-update) | async-done | bytes 1048592 | tf_op jit(solution)/shard_map/reduce_scatter | solution.py:175
  914.6 19.9 %all-reduce.1 = (f32[1024]{0:T(1024)S(1)}, f32[1024]{0:T(1024)S(1)}) all-reduce(f32[1024]{0:T(1024)S(1)} %get-tuple-element.326, f32[1024]{0:T(1024)S(1)} %get-tuple-element.325), channel_id=1, replica_groups=mesh['dp'=4,'wide'=8] {'wide'}, use_global_device_ids=true, to_apply=%region_26.27 | all-reduce | flops 2048 | bytes 16384 | tf_op jit(solution)/shard_map/psum | solution.py:151
  948.7 68.3 %all-gather.32.cloned.1.call-done = bf16[1024,2048]{1,0:T(8,128)(2,1)} async-done(((bf16[1024,256]{1,0:T(8,128)(2,1)}), bf16[1024,2048]{1,0:T(8,128)(2,1)}) %all-gather.32.cloned.1.call-update) | async-done | bytes 4194320 | tf_op jit(solution)/shard_map/all_gather | solution.py:155
  1020.7 30.5 %while.54 = (s32[]{:T(128)}, f32[1024,2,128]{0,2,1:T(8,128)S(1)}, f32[1024,2,128]{0,2,1:T(8,128)}, f32[2,512,2,128]{3,1,2,0:T(8,128)}, s32[2]{0:T(128)S(1)}, /*i...) while((s32[]{:T(128)}, f32[1024,2,128]{0,2,1:T(8,128)S(1)}, ...), condition=%wide.region_31.32_spmd.clone.clone, body=%wide.region_29.31_spmd.clone.sunk.clone | while | flops 1357250560 | bytes 90224648 | solution.py:144
  1135.9 76.0 %reduce-scatter.18.cloned.1.call-done = f32[1024,256]{1,0:T(8,128)} async-done(((f32[1024,2048]{1,0:T(8,128)}), f32[1024,256]{1,0:T(8,128)}) %reduce-scatter.18.cloned.1.call-update) | async-done | bytes 1048592 | tf_op jit(solution)/shard_map/reduce_scatter | solution.py:175
  1213.8 19.7 %all-reduce = (f32[1024]{0:T(1024)S(1)}, f32[1024]{0:T(1024)S(1)}) all-reduce(f32[1024]{0:T(1024)S(1)} %get-tuple-element.324, f32[1024]{0:T(1024)S(1)} %get-tuple-element.323), channel_id=1, replica_groups=mesh['dp'=4,'wide'=8] {'wide'}, use_global_device_ids=true, to_apply=%region_36.37 | all-reduce | flops 2048 | bytes 16384 | tf_op jit(solution)/shard_map/psum | solution.py:151
  1242.9 38.0 %psum.71 = f32[2,4,6]{2,1,0:T(4,128)} all-reduce(f32[2,4,6]{2,1,0:T(4,128)S(1)} %pad_maximum_fusion.3), channel_id=1, replica_groups=mesh['dp'=4,'wide'=8] {'dp','wide'}, use_global_device_ids=true, to_apply=%region_50.51 | all-reduce | flops 48 | bytes 384 | tf_op jit(solution)/shard_map/psum | solution.py:330
  1286.7 74.4 %reduce-scatter.28.cloned.1.call-done = f32[512,1024]{1,0:T(8,128)} async-done(((f32[2048,1024]{1,0:T(8,128)}), f32[512,1024]{1,0:T(8,128)}) %reduce-scatter.28.cloned.1.call-update) | async-done | bytes 2097168 | tf_op jit(solution)/shard_map/reduce_scatter | solution.py:264
  1361.1 74.4 %reduce-scatter.30.cloned.1.call-done = f32[512,1024]{1,0:T(8,128)} async-done(((f32[2048,1024]{1,0:T(8,128)}), f32[512,1024]{1,0:T(8,128)}) %reduce-scatter.30.cloned.1.call-update) | async-done | bytes 2097168 | tf_op jit(solution)/shard_map/reduce_scatter | solution.py:265
  1435.6 34.3 %reduce-scatter.22.cloned.1.call-done = f32[512,256]{1,0:T(8,128)} async-done(((f32[2048,256]{1,0:T(8,128)}), f32[512,256]{1,0:T(8,128)}) %reduce-scatter.22.cloned.1.call-update) | async-done | bytes 524304 | tf_op jit(solution)/shard_map/reduce_scatter | solution.py:341
  1469.9 34.2 %reduce-scatter.20.cloned.1.call-done = f32[512,256]{1,0:T(8,128)} async-done(((f32[2048,256]{1,0:T(8,128)}), f32[512,256]{1,0:T(8,128)}) %reduce-scatter.20.cloned.1.call-update) | async-done | bytes 524304 | tf_op jit(solution)/shard_map/reduce_scatter | solution.py:340
  1504.0 34.3 %reduce-scatter.26.cloned.1.call-done = f32[256,512]{1,0:T(8,128)} async-done(((f32[256,2048]{1,0:T(8,128)}), f32[256,512]{1,0:T(8,128)}) %reduce-scatter.26.cloned.1.call-update) | async-done | bytes 524304 | tf_op jit(solution)/shard_map/reduce_scatter | solution.py:343
  1538.4 34.3 %reduce-scatter.24.cloned.1.call-done = f32[512,256]{1,0:T(8,128)} async-done(((f32[2048,256]{1,0:T(8,128)}), f32[512,256]{1,0:T(8,128)}) %reduce-scatter.24.cloned.1.call-update) | async-done | bytes 524304 | tf_op jit(solution)/shard_map/reduce_scatter | solution.py:342
  (302 shorter events, 307.1 us)
Async XLA Ops:
  7.2 35.6 %all-gather.16.cloned.1.call-start = ((), (), s32[]{:S(2)}) async-start(), calls=%async_computation.13 | async-start | bytes 1310720 | tf_op jit(solution)/shard_map/all_gather | solution.py:209
  7.9 101.3 %all-gather.12.cloned.1.call-start = ((), (), s32[]{:S(2)}) async-start(), calls=%async_computation.11 | async-start | bytes 4718592 | tf_op jit(solution)/shard_map/all_gather | solution.py:155
  37.1 88.5 %all-gather.14.cloned.1.call-start = ((), (), s32[]{:S(2)}) async-start(), calls=%async_computation.12 | async-start | bytes 1310720 | tf_op jit(solution)/shard_map/all_gather | solution.py:208
  37.9 105.9 %all-gather.18.cloned.1.call-start = ((), (), s32[]{:S(2)}) async-start(), calls=%async_computation.14 | async-start | bytes 1310720 | tf_op jit(solution)/shard_map/all_gather | solution.py:210
  38.5 124.3 %all-gather.20.cloned.1.call-start = ((), (), s32[]{:S(2)}) async-start(), calls=%async_computation.15 | async-start | bytes 1310720 | tf_op jit(solution)/shard_map/all_gather | solution.py:211
  39.0 277.6 %reduce-scatter.12.cloned.1.call-start = ((), (), s32[]{:S(2)}) async-start(), calls=%async_computation.16 | async-start | bytes 9437184 | tf_op jit(solution)/shard_map/reduce_scatter | solution.py:159
  42.5 902.6 %copy-start.12 = (f32[1024,128]{0,1:T(8,128)}, f32[1024,128]{0,1:T(8,128)S(1)}, u32[]{:S(2)}) copy-start(f32[1024,128]{0,1:T(8,128)S(1)} %copy.61) | copy-start | bytes 1572868
  168.6 183.2 %all-gather.24.cloned.1.call-start = ((), (), s32[]{:S(2)}) async-start(), calls=%async_computation.18 | async-start | bytes 5242880 | tf_op jit(solution)/shard_map/all_gather | solution.py:214
  169.4 259.7 %all-gather.22.cloned.1.call-start = ((), (), s32[]{:S(2)}) async-start(), calls=%async_computation.17 | async-start | bytes 4718592 | tf_op jit(solution)/shard_map/all_gather | solution.py:155
  343.1 120.2 %all-gather.26.cloned.1.call-start = ((), (), s32[]{:S(2)}) async-start(), calls=%async_computation.19 | async-start | bytes 5242880 | tf_op jit(solution)/shard_map/all_gather | solution.py:215
  343.8 155.4 %all-gather.28.cloned.1.call-start = ((), (), s32[]{:S(2)}) async-start(), calls=%async_computation.20 | async-start | bytes 5242880 | tf_op jit(solution)/shard_map/all_gather | solution.py:216
  344.4 313.4 %reduce-scatter.14.cloned.1.call-start = ((), (), s32[]{:S(2)}) async-start(), calls=%async_computation.21 | async-start | bytes 9437184 | tf_op jit(solution)/shard_map/reduce_scatter | solution.py:159
  509.8 229.9 %all-gather.30.cloned.1.call-start = ((), (), s32[]{:S(2)}) async-start(), calls=%async_computation.22 | async-start | bytes 4718592 | tf_op jit(solution)/shard_map/all_gather | solution.py:155
  665.9 246.9 %reduce-scatter.16.cloned.1.call-start = ((), (), s32[]{:S(2)}) async-start(), calls=%async_computation.23 | async-start | bytes 9437184 | tf_op jit(solution)/shard_map/reduce_scatter | solution.py:175
  766.6 250.4 %all-gather.32.cloned.1.call-start = ((), (), s32[]{:S(2)}) async-start(), calls=%async_computation.24 | async-start | bytes 4718592 | tf_op jit(solution)/shard_map/all_gather | solution.py:155
  944.9 267.0 %reduce-scatter.18.cloned.1.call-start = ((), (), s32[]{:S(2)}) async-start(), calls=%async_computation.25 | async-start | bytes 9437184 | tf_op jit(solution)/shard_map/reduce_scatter | solution.py:175
  1065.7 221.0 %reduce-scatter.32.cloned.1.call-start = ((), (), s32[]{:S(2)}) async-start(), calls=%async_computation.32 | async-start | bytes 10485760 | tf_op jit(solution)/shard_map/reduce_scatter | solution.py:266
  1076.6 284.5 %reduce-scatter.28.cloned.1.call-start = ((), (), s32[]{:S(2)}) async-start(), calls=%async_computation.30 | async-start | bytes 10485760 | tf_op jit(solution)/shard_map/reduce_scatter | solution.py:264
  1087.4 348.2 %reduce-scatter.30.cloned.1.call-start = ((), (), s32[]{:S(2)}) async-start(), calls=%async_computation.31 | async-start | bytes 10485760 | tf_op jit(solution)/shard_map/reduce_scatter | solution.py:265
  1098.6 371.3 %reduce-scatter.22.cloned.1.call-start = ((), (), s32[]{:S(2)}) async-start(), calls=%async_computation.27 | async-start | bytes 2621440 | tf_op jit(solution)/shard_map/reduce_scatter | solution.py:341
  1103.5 400.5 %reduce-scatter.20.cloned.1.call-start = ((), (), s32[]{:S(2)}) async-start(), calls=%async_computation.26 | async-start | bytes 2621440 | tf_op jit(solution)/shard_map/reduce_scatter | solution.py:340
  1108.6 429.7 %reduce-scatter.26.cloned.1.call-start = ((), (), s32[]{:S(2)}) async-start(), calls=%async_computation.29 | async-start | bytes 2621440 | tf_op jit(solution)/shard_map/reduce_scatter | solution.py:343
  1113.9 458.8 %reduce-scatter.24.cloned.1.call-start = ((), (), s32[]{:S(2)}) async-start(), calls=%async_computation.28 | async-start | bytes 2621440 | tf_op jit(solution)/shard_map/reduce_scatter | solution.py:342
  1135.9 99.5 %copy-start.39 = (f32[4]{0:T(128)S(1)}, f32[4]{0:T(128)}, u32[]{:S(2)}) copy-start(f32[4]{0:T(128)} %copy-done.38) | copy-start | bytes 52
  (57 other events, 722.8 us)
Sparse Core Ops, SparseCore 0:
  9.5 19.4 all-gather.15
  37.3 71.8 all-gather.11
  110.8 14.8 all-gather.13
  127.1 16.6 all-gather.17
  145.2 16.6 all-gather.19
  168.7 147.8 reduce-scatter.11
  318.2 33.5 all-gather.23
  354.4 74.6 all-gather.21
  430.7 32.6 all-gather.25
  464.7 34.4 all-gather.27
  509.9 147.8 reduce-scatter.13
  666.0 73.7 all-gather.29
  766.7 146.0 reduce-scatter.15
  945.1 71.8 all-gather.31
  1065.9 146.0 reduce-scatter.17
  1214.9 71.7 reduce-scatter.31
  1289.7 71.3 reduce-scatter.27
  1364.1 71.3 reduce-scatter.29
  1438.7 31.1 reduce-scatter.21
  1472.8 31.1 reduce-scatter.19
  1507.2 31.1 reduce-scatter.25
  1541.5 31.1 reduce-scatter.23
where the time goes:
time: 1590 us; the launch traced here: 1580 us
  waiting for transfers between devices  1160 us (73%)
  matrix products  165 us (10%)
  blocking collectives  127 us (8%)
  other arithmetic  86.2 us (5%)
  local copies, waits for them, and re-layouts  21 us (1%)
    all_gather x4, waiting for transfers between devices, features(): return lax.all_gather(piece, 'wide', axis=1, tiled=True)  285 us
    reduce_scatter x2, waiting for transfers between devices, branch_rows(): lax.psum_scatter(partial_value, 'wide', scatter_dimension=1, tiled=True)  278 us
    reduce_scatter x2, waiting for transfers between devices, norm_backward(): lax.psum_scatter(partial_value, 'wide', scatter_dimension=1, tiled=True)  222 us
    psum x4, blocking collectives, row_sums(): lax.psum((jnp.sum(first_term, axis=1), jnp.sum(second_term, axis=1)), 'wi...  82.8 us
    reduce_scatter x1, waiting for transfers between devices, per_device(): lax.psum_scatter(up_wgrad, 'dp', scatter_dimension=0, tiled=True)  74.4 us
    reduce_scatter x1, waiting for transfers between devices, per_device(): lax.psum_scatter(gate_wgrad, 'dp', scatter_dimension=0, tiled=True)  74.4 us
    psum x1, blocking collectives, per_device(): lax.psum(jnp.stack([hyper_rows(attn_pre_grad, attn_post_grad, attn_mix_gr...  38 us
    reduce_scatter x1, waiting for transfers between devices, per_device(): lax.psum_scatter(out_wgrad, 'dp', scatter_dimension=1, tiled=True)  34.3 us
  transfers between devices with their start and end apart: 22, of which 20 were waited for; matrix products, arithmetic and copies ran while one was open for 10% of the time, Pallas kernels for 0%

commit v1 on v0

--- a/solution.py
+++ b/solution.py
@@ -9,6 +9,18 @@
 CLIP_TAU = 6
 EPSILON = 1e-05
 MASKED = -1e30
+
+
+def doubled_up(shard, axis, dim):
+    ways, here = (lax.axis_size(axis), lax.axis_index(axis))
+    grown, reach = (shard, 1)
+    while reach < ways:
+        theirs = lax.ppermute(grown, axis, [(d, d ^ reach) for d in range(ways)])
+        mine_first = jnp.concatenate([grown, theirs], axis=dim)
+        theirs_first = jnp.concatenate([theirs, grown], axis=dim)
+        grown = jnp.where(here & reach == 0, mine_first, theirs_first)
+        reach = 2 * reach
+    return grown
 
 
 def rope_tables(length, head_size):
@@ -152,7 +164,7 @@
 
 
 def features(piece):
-    return lax.all_gather(piece, "wide", axis=1, tiled=True)
+    return doubled_up(piece, "wide", 1)
 
 
 def branch_rows(partial_value):

time: 1590 us -> 1700 us (1.069)
  waiting for transfers between devices: 1160 us -> 1250 us
    ppermute x0 -> x12, waiting for transfers between devices: none -> 470 us  [doubled_up(): theirs = lax.ppermute(grown, axis, [(d, d ^ reach) for d in range(ways)])]
    all_gather x4 -> x0, waiting for transfers between devices: 285 us -> none  [features(): return lax.all_gather(piece, 'wide', axis=1, tiled=True)]
    all_gather x1, waiting for transfers between devices: 24.3 us -> 0.01 us  [per_device(): lax.all_gather(w_up, 'dp', axis=0, tiled=True)]
    all_gather x1, waiting for transfers between devices: 23.8 us -> 0.01 us  [per_device(): lax.all_gather(w_down, 'dp', axis=1, tiled=True)]
  transfers between devices with their start and end apart: 22 -> 30, of which waited for: 20 -> 23; matrix products, arithmetic and copies ran while one was open for 10% -> 10% of each run, Pallas kernels for 0% -> 0%
where the time goes in v1:
time: 1700 us
  waiting for transfers between devices  1250 us (74%)
  matrix products  169 us (10%)
  blocking collectives  128 us (8%)
  other arithmetic  98.7 us (6%)
  local copies, waits for them, and re-layouts  22.8 us (1%)
    ppermute x12, waiting for transfers between devices, doubled_up(): theirs = lax.ppermute(grown, axis, [(d, d ^ reach) for d in range(ways)])  470 us
    reduce_scatter x2, waiting for transfers between devices, branch_rows(): lax.psum_scatter(partial_value, 'wide', scatter_dimension=1, tiled=True)  271 us
    reduce_scatter x2, waiting for transfers between devices, norm_backward(): lax.psum_scatter(partial_value, 'wide', scatter_dimension=1, tiled=True)  217 us
    psum x4, blocking collectives, row_sums(): lax.psum((jnp.sum(first_term, axis=1), jnp.sum(second_term, axis=1)), 'wi...  82.8 us
    reduce_scatter x1, waiting for transfers between devices, per_device(): lax.psum_scatter(up_wgrad, 'dp', scatter_dimension=0, tiled=True)  74.6 us
    reduce_scatter x1, waiting for transfers between devices, per_device(): lax.psum_scatter(gate_wgrad, 'dp', scatter_dimension=0, tiled=True)  74.4 us
    psum x1, blocking collectives, per_device(): lax.psum(jnp.stack([hyper_rows(attn_pre_grad, attn_post_grad, attn_mix_gr...  38 us
    reduce_scatter x1, waiting for transfers between devices, per_device(): lax.psum_scatter(key_wgrad, 'dp', scatter_dimension=0, tiled=True)  34.2 us
  transfers between devices with their start and end apart: 30, of which 23 were waited for; matrix products, arithmetic and copies ran while one was open for 10% of the time, Pallas kernels for 0%

profile of v1, /device:TPU:0, one launch (start us, length us, event | category | flops | bytes accessed | tf_op | source)
XLA Modules:
  0.0 1696.5 jit_solution(12485429996054742657)
XLA Ops:
  12.7 23.5 %all-reduce.3 = (f32[1024]{0:T(1024)S(1)}, f32[1024]{0:T(1024)S(1)}) all-reduce(f32[1024]{0:T(1024)S(1)} %multiply_reduce_fusion.20, f32[1024]{0:T(1024)S(1)} %get-tuple-element.312), channel_id=1, replica_groups=mesh['dp'=4,'wide'=8] {'wide'}, use_global_device_ids=true, to_apply=%region_5.6 | all-reduce | flops 2048 | bytes 16384 | tf_op jit(solution)/shard_map/psum | solution.py:163
  47.8 19.6 %collective-permute-done.1 = bf16[1024,512]{1,0:T(8,128)(2,1)} collective-permute-done((bf16[1024,512]{1,0:T(8,128)(2,1)S(1)}, bf16[1024,512]{1,0:T(8,128)(2,1)}, u32[]{:S(2)}, u32[]{:S(2)}) %collective-permute-start.1) | collective-permute-done | bytes 1048608 | tf_op jit(solution)/shard_map/ppermute | solution.py:18
  76.3 82.1 %collective-permute-done.2 = bf16[1024,1024]{1,0:T(8,128)(2,1)} collective-permute-done((bf16[1024,1024]{1,0:T(8,128)(2,1)S(1)}, bf16[1024,1024]{1,0:T(8,128)(2,1)}, u32[]{:S(2)}, u32[]{:S(2)}) %collective-permute-start.2) | collective-permute-done | bytes 2097184 | tf_op jit(solution)/shard_map/ppermute | solution.py:18
  205.9 137.6 %reduce-scatter.12.cloned.1.call-done = f32[1024,256]{1,0:T(8,128)} async-done(((f32[1024,2048]{1,0:T(8,128)}), f32[1024,256]{1,0:T(8,128)}) %reduce-scatter.12.cloned.1.call-update) | async-done | bytes 1048592 | tf_op jit(solution)/shard_map/reduce_scatter | solution.py:171
  349.0 19.8 %all-reduce.2 = (f32[1024]{0:T(1024)S(1)}, f32[1024]{0:T(1024)S(1)}) all-reduce(f32[1024]{0:T(1024)S(1)} %multiply_reduce_fusion.19, f32[1024]{0:T(1024)S(1)} %get-tuple-element.310), channel_id=1, replica_groups=mesh['dp'=4,'wide'=8] {'wide'}, use_global_device_ids=true, to_apply=%region_18.19 | all-reduce | flops 2048 | bytes 16384 | tf_op jit(solution)/shard_map/psum | solution.py:163
  381.0 20.5 %collective-permute-done.4 = bf16[1024,512]{1,0:T(8,128)(2,1)S(1)} collective-permute-done((bf16[1024,512]{1,0:T(8,128)(2,1)S(1)}, bf16[1024,512]{1,0:T(8,128)(2,1)S(1)}, u32[]{:S(2)}, u32[]{:S(2)}) %collective-permute-start.4) | collective-permute-done | bytes 1048608 | tf_op jit(solution)/shard_map/ppermute | solution.py:18
  403.5 88.4 %collective-permute-done.5 = bf16[1024,1024]{1,0:T(8,128)(2,1)} collective-permute-done((bf16[1024,1024]{1,0:T(8,128)(2,1)}, bf16[1024,1024]{1,0:T(8,128)(2,1)}, u32[]{:S(2)}, u32[]{:S(2)}) %collective-permute-start.5) | collective-permute-done | bytes 2097184 | tf_op jit(solution)/shard_map/ppermute | solution.py:18
  536.1 133.6 %reduce-scatter.14.cloned.1.call-done = f32[1024,256]{1,0:T(8,128)} async-done(((f32[1024,2048]{1,0:T(8,128)}), f32[1024,256]{1,0:T(8,128)}) %reduce-scatter.14.cloned.1.call-update) | async-done | bytes 1048592 | tf_op jit(solution)/shard_map/reduce_scatter | solution.py:171
  691.4 23.4 %collective-permute-done.7 = bf16[1024,512]{1,0:T(8,128)(2,1)S(1)} collective-permute-done((bf16[1024,512]{1,0:T(8,128)(2,1)S(1)}, bf16[1024,512]{1,0:T(8,128)(2,1)S(1)}, u32[]{:S(2)}, u32[]{:S(2)}) %collective-permute-start.7) | collective-permute-done | bytes 1048608 | tf_op jit(solution)/shard_map/ppermute | solution.py:18
  717.4 89.2 %collective-permute-done.8 = bf16[1024,1024]{1,0:T(8,128)(2,1)S(1)} collective-permute-done((bf16[1024,1024]{1,0:T(8,128)(2,1)S(1)}, bf16[1024,1024]{1,0:T(8,128)(2,1)S(1)}, u32[]{:S(2)}, u32[]{:S(2)}) %collective-permute-start.8) | collective-permute-done | bytes 2097184 | tf_op jit(solution)/shard_map/ppermute | solution.py:18
  831.6 148.7 %reduce-scatter.16.cloned.1.call-done = f32[1024,256]{1,0:T(8,128)} async-done(((f32[1024,2048]{1,0:T(8,128)}), f32[1024,256]{1,0:T(8,128)}) %reduce-scatter.16.cloned.1.call-update) | async-done | bytes 1048592 | tf_op jit(solution)/shard_map/reduce_scatter | solution.py:187
  982.1 19.7 %all-reduce.1 = (f32[1024]{0:T(1024)S(1)}, f32[1024]{0:T(1024)S(1)}) all-reduce(f32[1024]{0:T(1024)S(1)} %get-tuple-element.326, f32[1024]{0:T(1024)S(1)} %get-tuple-element.325), channel_id=1, replica_groups=mesh['dp'=4,'wide'=8] {'wide'}, use_global_device_ids=true, to_apply=%region_26.27 | all-reduce | flops 2048 | bytes 16384 | tf_op jit(solution)/shard_map/psum | solution.py:163
  1021.9 20.5 %collective-permute-done.10 = bf16[1024,512]{1,0:T(8,128)(2,1)S(1)} collective-permute-done((bf16[1024,512]{1,0:T(8,128)(2,1)S(1)}, bf16[1024,512]{1,0:T(8,128)(2,1)S(1)}, u32[]{:S(2)}, u32[]{:S(2)}) %collective-permute-start.10) | collective-permute-done | bytes 1048608 | tf_op jit(solution)/shard_map/ppermute | solution.py:18
  1048.1 84.7 %collective-permute-done.11 = bf16[1024,1024]{1,0:T(8,128)(2,1)} collective-permute-done((bf16[1024,1024]{1,0:T(8,128)(2,1)}, bf16[1024,1024]{1,0:T(8,128)(2,1)}, u32[]{:S(2)}, u32[]{:S(2)}) %collective-permute-start.11) | collective-permute-done | bytes 2097184 | tf_op jit(solution)/shard_map/ppermute | solution.py:18
  1138.0 30.9 %while.54 = (s32[]{:T(128)}, f32[1024,2,128]{0,2,1:T(8,128)S(1)}, f32[1024,2,128]{0,2,1:T(8,128)}, f32[2,512,2,128]{3,1,2,0:T(8,128)}, s32[2]{0:T(128)S(1)}, /*i...) while((s32[]{:T(128)}, f32[1024,2,128]{0,2,1:T(8,128)S(1)}, ...), condition=%wide.region_31.32_spmd.clone.clone, body=%wide.region_29.31_spmd.clone.sunk.clone | while | flops 1357250560 | bytes 90224648 | solution.py:156
  1260.8 68.2 %reduce-scatter.18.cloned.1.call-done = f32[1024,256]{1,0:T(8,128)} async-done(((f32[1024,2048]{1,0:T(8,128)}), f32[1024,256]{1,0:T(8,128)}) %reduce-scatter.18.cloned.1.call-update) | async-done | bytes 1048592 | tf_op jit(solution)/shard_map/reduce_scatter | solution.py:187
  1330.9 19.7 %all-reduce = (f32[1024]{0:T(1024)S(1)}, f32[1024]{0:T(1024)S(1)}) all-reduce(f32[1024]{0:T(1024)S(1)} %get-tuple-element.324, f32[1024]{0:T(1024)S(1)} %get-tuple-element.323), channel_id=1, replica_groups=mesh['dp'=4,'wide'=8] {'wide'}, use_global_device_ids=true, to_apply=%region_36.37 | all-reduce | flops 2048 | bytes 16384 | tf_op jit(solution)/shard_map/psum | solution.py:163
  1359.9 38.0 %psum.71 = f32[2,4,6]{2,1,0:T(4,128)} all-reduce(f32[2,4,6]{2,1,0:T(4,128)S(1)} %pad_maximum_fusion.3), channel_id=1, replica_groups=mesh['dp'=4,'wide'=8] {'dp','wide'}, use_global_device_ids=true, to_apply=%region_50.51 | all-reduce | flops 48 | bytes 384 | tf_op jit(solution)/shard_map/psum | solution.py:342
  1403.8 74.6 %reduce-scatter.30.cloned.1.call-done = f32[512,1024]{1,0:T(8,128)} async-done(((f32[2048,1024]{1,0:T(8,128)}), f32[512,1024]{1,0:T(8,128)}) %reduce-scatter.30.cloned.1.call-update) | async-done | bytes 2097168 | tf_op jit(solution)/shard_map/reduce_scatter | solution.py:277
  1478.3 74.4 %reduce-scatter.28.cloned.1.call-done = f32[512,1024]{1,0:T(8,128)} async-done(((f32[2048,1024]{1,0:T(8,128)}), f32[512,1024]{1,0:T(8,128)}) %reduce-scatter.28.cloned.1.call-update) | async-done | bytes 2097168 | tf_op jit(solution)/shard_map/reduce_scatter | solution.py:276
  1552.8 34.2 %reduce-scatter.26.cloned.1.call-done = f32[256,512]{1,0:T(8,128)} async-done(((f32[256,2048]{1,0:T(8,128)}), f32[256,512]{1,0:T(8,128)}) %reduce-scatter.26.cloned.1.call-update) | async-done | bytes 524304 | tf_op jit(solution)/shard_map/reduce_scatter | solution.py:355
  1586.9 34.2 %reduce-scatter.22.cloned.1.call-done = f32[512,256]{1,0:T(8,128)} async-done(((f32[2048,256]{1,0:T(8,128)}), f32[512,256]{1,0:T(8,128)}) %reduce-scatter.22.cloned.1.call-update) | async-done | bytes 524304 | tf_op jit(solution)/shard_map/reduce_scatter | solution.py:353
  1621.1 34.2 %reduce-scatter.20.cloned.1.call-done = f32[512,256]{1,0:T(8,128)} async-done(((f32[2048,256]{1,0:T(8,128)}), f32[512,256]{1,0:T(8,128)}) %reduce-scatter.20.cloned.1.call-update) | async-done | bytes 524304 | tf_op jit(solution)/shard_map/reduce_scatter | solution.py:352
  1655.3 34.2 %reduce-scatter.24.cloned.1.call-done = f32[512,256]{1,0:T(8,128)} async-done(((f32[2048,256]{1,0:T(8,128)}), f32[512,256]{1,0:T(8,128)}) %reduce-scatter.24.cloned.1.call-update) | async-done | bytes 524304 | tf_op jit(solution)/shard_map/reduce_scatter | solution.py:354
  (331 shorter events, 368.3 us)
Async XLA Ops:
  7.2 156.6 %all-gather.10.cloned.1.call-start = ((), (), s32[]{:S(2)}) async-start(), calls=%async_computation.12 | async-start | bytes 1310720 | tf_op jit(solution)/shard_map/all_gather | solution.py:221
  7.9 160.6 %all-gather.8.cloned.1.call-start = ((), (), s32[]{:S(2)}) async-start(), calls=%async_computation.11 | async-start | bytes 1310720 | tf_op jit(solution)/shard_map/all_gather | solution.py:220
  8.7 165.2 %all-gather.12.cloned.1.call-start = ((), (), s32[]{:S(2)}) async-start(), calls=%async_computation.13 | async-start | bytes 1310720 | tf_op jit(solution)/shard_map/all_gather | solution.py:222
  46.9 145.4 %all-gather.14.cloned.1.call-start = ((), (), s32[]{:S(2)}) async-start(), calls=%async_computation.14 | async-start | bytes 1310720 | tf_op jit(solution)/shard_map/all_gather | solution.py:223
  70.4 88.0 %collective-permute-start.2 = (bf16[1024,1024]{1,0:T(8,128)(2,1)S(1)}, bf16[1024,1024]{1,0:T(8,128)(2,1)}, u32[]{:S(2)}, u32[]{:S(2)}) collective-permute-start(bf16[1024,1024]{1,0:T(8,128)(2,1)S(1)} %maximum_select_fusion.4), channel_id=1, source_target_pairs={{0,4},{1,5},{2,6},{3,7},{4,0},{5,1},{6,2},{7,3},{8,12},{9,13},{10,... | collective-permute-start | bytes 6291464 | tf_op jit(solution)/shard_map/ppermute | solution.py:18
  70.5 273.0 %reduce-scatter.12.cloned.1.call-start = ((), (), s32[]{:S(2)}) async-start(), calls=%async_computation.15 | async-start | bytes 9437184 | tf_op jit(solution)/shard_map/reduce_scatter | solution.py:171
  198.2 205.3 %all-gather.16.cloned.1.call-start = ((), (), s32[]{:S(2)}) async-start(), calls=%async_computation.16 | async-start | bytes 5242880 | tf_op jit(solution)/shard_map/all_gather | solution.py:226
  198.8 304.3 %all-gather.18.cloned.1.call-start = ((), (), s32[]{:S(2)}) async-start(), calls=%async_computation.17 | async-start | bytes 5242880 | tf_op jit(solution)/shard_map/all_gather | solution.py:227
  199.5 314.2 %all-gather.20.cloned.1.call-start = ((), (), s32[]{:S(2)}) async-start(), calls=%async_computation.18 | async-start | bytes 5242880 | tf_op jit(solution)/shard_map/all_gather | solution.py:228
  369.3 300.5 %reduce-scatter.14.cloned.1.call-start = ((), (), s32[]{:S(2)}) async-start(), calls=%async_computation.19 | async-start | bytes 9437184 | tf_op jit(solution)/shard_map/reduce_scatter | solution.py:171
  403.5 88.4 %collective-permute-start.5 = (bf16[1024,1024]{1,0:T(8,128)(2,1)}, bf16[1024,1024]{1,0:T(8,128)(2,1)}, u32[]{:S(2)}, u32[]{:S(2)}) collective-permute-start(bf16[1024,1024]{1,0:T(8,128)(2,1)} %maximum_select_fusion.5), channel_id=1, source_target_pairs={{0,4},{1,5},{2,6},{3,7},{4,0},{5,1},{6,2},{7,3},{8,12},{9,13},{10,... | collective-permute-start | bytes 6291464 | tf_op jit(solution)/shard_map/ppermute | solution.py:18
  524.3 456.0 %reduce-scatter.16.cloned.1.call-start = ((), (), s32[]{:S(2)}) async-start(), calls=%async_computation.20 | async-start | bytes 9437184 | tf_op jit(solution)/shard_map/reduce_scatter | solution.py:187
  690.9 23.8 %collective-permute-start.7 = (bf16[1024,512]{1,0:T(8,128)(2,1)S(1)}, bf16[1024,512]{1,0:T(8,128)(2,1)S(1)}, u32[]{:S(2)}, u32[]{:S(2)}) collective-permute-start(bf16[1024,512]{1,0:T(8,128)(2,1)S(1)} %maximum_select_fusion.10), channel_id=1, source_target_pairs={{0,2},{1,3},{2,0},{3,1},{4,6},{5,7},{6,4},{7,5},{8,10},{9,11},{10,... | collective-permute-start | bytes 3145736 | tf_op jit(solution)/shard_map/ppermute | solution.py:18
  715.4 91.3 %collective-permute-start.8 = (bf16[1024,1024]{1,0:T(8,128)(2,1)S(1)}, bf16[1024,1024]{1,0:T(8,128)(2,1)S(1)}, u32[]{:S(2)}, u32[]{:S(2)}) collective-permute-start(bf16[1024,1024]{1,0:T(8,128)(2,1)S(1)} %maximum_select_fusion.6), channel_id=1, source_target_pairs={{0,4},{1,5},{2,6},{3,7},{4,0},{5,1},{6,2},{7,3},{8,12},{9,13},{10,... | collective-permute-start | bytes 6291464 | tf_op jit(solution)/shard_map/ppermute | solution.py:18
  831.6 497.4 %reduce-scatter.18.cloned.1.call-start = ((), (), s32[]{:S(2)}) async-start(), calls=%async_computation.21 | async-start | bytes 9437184 | tf_op jit(solution)/shard_map/reduce_scatter | solution.py:187
  1021.8 20.6 %collective-permute-start.10 = (bf16[1024,512]{1,0:T(8,128)(2,1)S(1)}, bf16[1024,512]{1,0:T(8,128)(2,1)S(1)}, u32[]{:S(2)}, u32[]{:S(2)}) collective-permute-start(bf16[1024,512]{1,0:T(8,128)(2,1)S(1)} %maximum_select_fusion.11), channel_id=1, source_target_pairs={{0,2},{1,3},{2,0},{3,1},{4,6},{5,7},{6,4},{7,5},{8,10},{9,11},{10,... | collective-permute-start | bytes 3145736 | tf_op jit(solution)/shard_map/ppermute | solution.py:18
  1044.4 88.3 %collective-permute-start.11 = (bf16[1024,1024]{1,0:T(8,128)(2,1)}, bf16[1024,1024]{1,0:T(8,128)(2,1)}, u32[]{:S(2)}, u32[]{:S(2)}) collective-permute-start(bf16[1024,1024]{1,0:T(8,128)(2,1)} %maximum_select_fusion.7), channel_id=1, source_target_pairs={{0,4},{1,5},{2,6},{3,7},{4,0},{5,1},{6,2},{7,3},{8,12},{9,13},{10,... | collective-permute-start | bytes 6291464 | tf_op jit(solution)/shard_map/ppermute | solution.py:18
  1183.4 220.4 %reduce-scatter.32.cloned.1.call-start = ((), (), s32[]{:S(2)}) async-start(), calls=%async_computation.28 | async-start | bytes 10485760 | tf_op jit(solution)/shard_map/reduce_scatter | solution.py:278
  1195.4 283.0 %reduce-scatter.30.cloned.1.call-start = ((), (), s32[]{:S(2)}) async-start(), calls=%async_computation.27 | async-start | bytes 10485760 | tf_op jit(solution)/shard_map/reduce_scatter | solution.py:277
  1207.8 345.0 %reduce-scatter.28.cloned.1.call-start = ((), (), s32[]{:S(2)}) async-start(), calls=%async_computation.26 | async-start | bytes 10485760 | tf_op jit(solution)/shard_map/reduce_scatter | solution.py:276
  1220.1 366.9 %reduce-scatter.26.cloned.1.call-start = ((), (), s32[]{:S(2)}) async-start(), calls=%async_computation.25 | async-start | bytes 2621440 | tf_op jit(solution)/shard_map/reduce_scatter | solution.py:355
  1227.6 393.5 %reduce-scatter.22.cloned.1.call-start = ((), (), s32[]{:S(2)}) async-start(), calls=%async_computation.23 | async-start | bytes 2621440 | tf_op jit(solution)/shard_map/reduce_scatter | solution.py:353
  1232.6 422.7 %reduce-scatter.20.cloned.1.call-start = ((), (), s32[]{:S(2)}) async-start(), calls=%async_computation.22 | async-start | bytes 2621440 | tf_op jit(solution)/shard_map/reduce_scatter | solution.py:352
  1237.8 451.7 %reduce-scatter.24.cloned.1.call-start = ((), (), s32[]{:S(2)}) async-start(), calls=%async_computation.24 | async-start | bytes 2621440 | tf_op jit(solution)/shard_map/reduce_scatter | solution.py:354
  (69 other events, 1229.6 us)
Sparse Core Ops, SparseCore 0:
  9.5 19.4 all-gather.9
  30.6 16.6 all-gather.7
  48.9 16.6 all-gather.11
  70.6 16.2 all-gather.13
  198.3 145.1 reduce-scatter.11
  344.9 33.5 all-gather.15
  380.0 34.4 all-gather.17
  416.1 34.4 all-gather.19
  524.4 145.3 reduce-scatter.13
  831.7 148.5 reduce-scatter.15
  1183.5 145.4 reduce-scatter.17
  1332.0 71.7 reduce-scatter.31
  1406.9 71.3 reduce-scatter.29
  1481.4 71.3 reduce-scatter.27
  1555.7 31.1 reduce-scatter.25
  1589.9 31.1 reduce-scatter.21
  1624.1 31.1 reduce-scatter.19
  1658.2 31.1 reduce-scatter.23
